TPU v7x, 32 devices: a whole 2x2x4 slice. The times are simulated.
32 devices in a mesh: band: 8 (over z, x), sub: 4 (over y, core).
Axes of the slice: x: 2, y: 2, z: 4, core: 2. Of those that a mesh axis runs over, the one named last changes fastest.
Arguments:
- grad_pred: bfloat16 [227, 24576], P(None, ('band', 'sub')), may hold values from -6 to 6
- grid_latent: bfloat16 [24576, 512], P(('band', 'sub')), may hold values from -6 to 6
- mesh_latent: bfloat16 [10240, 512], P(('band', 'sub')), may hold values from -6 to 6
- send_slot: int32 [24576], P(('band', 'sub')), may hold values from 0 to 2303, as said below
- edge_src: int32 [3, 73728], P(None, ('band', 'sub')), may hold values from 0 to 10239, as said below
- w_mesh: bfloat16 [512, 512], replicated, may hold values from -0.25 to 0.25
- w_grid: bfloat16 [512, 512], replicated, may hold values from -0.25 to 0.25
- w_msg: bfloat16 [512, 512], replicated, may hold values from -0.25 to 0.25
- w_out: bfloat16 [512, 227], replicated, may hold values from -0.25 to 0.25
Outputs:
- mesh_grad: bfloat16 [10240, 512], P(('band', 'sub'))
- grad_w_mesh: float32 [512, 512], replicated
- grad_w_grid: float32 [512, 512], replicated
- grad_w_msg: float32 [512, 512], replicated
- grad_w_out: float32 [512, 227], replicated
Inputs may be any that keep to these rules, and one draw needn't show every extreme that they name: For grid point p on latitude-major device i, send_slot[p] = j * 72 + r names patch-major device j and a rank r. On one device i the values are distinct, and for each j the ranks used are 0 to the count of i's points sent to j minus 1. Every such count is at most 72, and 72 is reached in every draw. Every grid point thereby gets one patch-major slot; live slots of each source stand at the front of its block of 72. One patch-major device holds at most 1920 live slots, reached on some device in every draw. `edge_src`: A slot on patch-major device j, of band b = j // 4, names senders in patch b only: mesh rows b * 1280 to (b + 1) * 1280 - 1. Entries of empty slots lie in that range too and are not read.
All inputs are finite; a program needn't handle non-finite values.
Results may differ from a plain program's by a relative error of at most 0.0076.
Values may be sent and summed in bfloat16 or wider, within the bound.
No kernel may reach another device: no remote copies, remote signals or barrier semaphores. Data moves between devices by JAX's collectives and lax.ppermute only.
A program may use at most 128 MiB of HBM per device.

v0:
```python
import math
import jax
import jax.numpy as jnp
from jax import lax
from jax.sharding import PartitionSpec as P


def latitude_weight(points, total):
    angle = jnp.pi * ((points.astype(jnp.float32) + 0.5) / total - 0.5)
    return 0.5 * jnp.pi * jnp.cos(angle)


def silu_slope(value):
    sigma = jax.nn.sigmoid(value)
    return sigma * (1.0 + value * (1.0 - sigma))


def contract_rows(left, right):
    return lax.dot_general(
        left, right, (((0,), (0,)), ((), ())), preferred_element_type=jnp.float32
    )


def times_transpose(left, right):
    return lax.dot_general(
        left, right, (((1,), (1,)), ((), ())), preferred_element_type=jnp.float32
    )


def shards(grad_pred, grid_latent, mesh_latent, send_slot, edge_src, w_mesh, w_grid, w_msg, w_out):
    grid_rows = grid_latent.shape[0]
    width = grid_latent.shape[1]
    channels = grad_pred.shape[0]
    devices = lax.axis_size(("band", "sub"))
    capacity = 3 * grid_rows // devices
    total_points = grid_rows * devices
    own_index = lax.axis_index(("band", "sub"))
    points = own_index * grid_rows + jnp.arange(grid_rows, dtype=jnp.int32)
    weighted = (
        latitude_weight(points, total_points)[None, :] * grad_pred.astype(jnp.float32)
    ).astype(jnp.bfloat16)
    target = send_slot // capacity
    slot_rank = send_slot % capacity
    joined = jnp.concatenate([grid_latent, weighted.T], axis=1)
    row_width = width + channels
    send_buffer = (
        jnp.zeros((devices, capacity, row_width), jnp.bfloat16).at[target, slot_rank].set(joined)
    )
    received = lax.all_to_all(send_buffer, ("band", "sub"), split_axis=0, concat_axis=0, tiled=True)
    slots = devices * capacity
    slot_rows = received.reshape(slots, row_width)
    latent_rows = slot_rows[:, :width]
    grad_rows = slot_rows[:, width:]
    grid_proj = jnp.dot(latent_rows, w_grid, preferred_element_type=jnp.float32).astype(
        jnp.bfloat16
    )
    mesh_proj = jnp.dot(mesh_latent, w_mesh, preferred_element_type=jnp.float32).astype(
        jnp.bfloat16
    )
    patch_proj = lax.all_gather(mesh_proj, "sub", axis=0, tiled=True)
    patch_size = patch_proj.shape[0]
    band_index = lax.axis_index("band")
    local_node = edge_src - band_index * patch_size
    grid_float = grid_proj.astype(jnp.float32)
    pre_acts = [
        patch_proj[local_node[corner]].astype(jnp.float32) + grid_float for corner in range(3)
    ]
    act_sum = (
        jax.nn.silu(pre_acts[0]) + jax.nn.silu(pre_acts[1]) + jax.nn.silu(pre_acts[2])
    ).astype(jnp.bfloat16)
    aggregate = jnp.dot(act_sum, w_msg, preferred_element_type=jnp.float32).astype(jnp.bfloat16)
    out_part = contract_rows(aggregate, grad_rows)
    agg_rows = times_transpose(grad_rows, w_out).astype(jnp.bfloat16)
    msg_part = contract_rows(act_sum, agg_rows)
    out_total = lax.psum(out_part, ("band", "sub"))
    msg_total = lax.psum(msg_part, ("band", "sub"))
    act_grad = times_transpose(agg_rows, w_msg)
    pre_grads = [(act_grad * silu_slope(pre)).astype(jnp.bfloat16) for pre in pre_acts]
    grid_proj_grad = (
        pre_grads[0].astype(jnp.float32)
        + pre_grads[1].astype(jnp.float32)
        + pre_grads[2].astype(jnp.float32)
    ).astype(jnp.bfloat16)
    node_part = jnp.zeros((patch_size, width), jnp.float32)
    for corner in range(3):
        node_part = node_part.at[local_node[corner]].add(pre_grads[corner].astype(jnp.float32))
    node_total = lax.psum_scatter(node_part, "sub", scatter_dimension=0, tiled=True)
    grid_part = contract_rows(latent_rows, grid_proj_grad)
    mesh_proj_grad = node_total.astype(jnp.bfloat16)
    mesh_grad = times_transpose(mesh_proj_grad, w_mesh).astype(jnp.bfloat16)
    mesh_part = contract_rows(mesh_latent, mesh_proj_grad)
    grad_scale = 1.0 / math.sqrt(3.0 * total_points)
    grid_total = lax.psum(grid_part, ("band", "sub"))
    mesh_total = lax.psum(mesh_part, ("band", "sub"))
    return (
        mesh_grad,
        mesh_total * grad_scale,
        grid_total * grad_scale,
        msg_total * grad_scale,
        out_total * grad_scale,
    )


def solution(mesh):
    placed = (
        P(None, ("band", "sub")),
        P(("band", "sub"), None),
        P(("band", "sub"), None),
        P(("band", "sub")),
        P(None, ("band", "sub")),
        P(),
        P(),
        P(),
        P(),
    )
    return jax.shard_map(
        shards,
        mesh=mesh,
        in_specs=placed,
        out_specs=(P(("band", "sub"), None), P(), P(), P(), P()),
        check_vma=False,
    )
```

profile of v0, /device:TPU:0, one launch (start us, length us, event | category | flops | bytes accessed | tf_op | source)
XLA Modules:
  0.0 467.4 jit_solution(4389432427457058807)
XLA Ops:
  7.2 0.0 copy-start
  7.2 0.8 compare_select_fusion.4
  8.0 1.0 fusion.15
  9.0 0.2 copy.26
  9.2 1.2 pad_maximum_fusion
  10.5 2.0 broadcast_in_dim.9
  12.5 101.6 %scatter_fusion = bf16[32,72,739]{2,1,0:T(8,128)(2,1)} fusion(bf16[32,72,739]{2,1,0:T(8,128)(2,1)} %broadcast_in_dim.9, s32[768]{0:T(1024)S(1)} %fusion.23, bf16[768,739]{1,0:T(8,128)(2,1)S(1)} %pad_maximum_fusion), kind=kCustom, calls=%fused_computation.3 | custom fusion | bytes 3411456 | tf_op jit(solution)/shard_map/scatter | solution.py:47
  114.1 7.4 %all-to-all-start = ((bf16[32,72,739]{2,1,0:T(8,128)(2,1)}), bf16[32,72,739]{2,1,0:T(8,128)(2,1)}, u32[]{:S(2)}, u32[]{:S(2)}) async-start(bf16[32,72,739]{2,1,0:T(8,128)(2,1)} %scatter_fusion), calls=%async_computation | async-start | bytes 7077888 | tf_op jit(solution)/shard_map/all_to_all | solution.py:49
  121.6 0.0 all-gather.2.cloned.1.call-start
  121.6 1.1 convolution_convert_fusion.4
  122.7 0.0 all-gather.2.cloned.1.call-update
  122.7 0.0 reduce-scatter.2.cloned.1.call-start
  122.8 0.1 fusion.20
  122.9 33.9 %all-gather.2.cloned.1.call-done = bf16[1280,512]{1,0:T(8,128)(2,1)} async-done(((bf16[320,512]{1,0:T(8,128)(2,1)}), bf16[1280,512]{1,0:T(8,128)(2,1)}) %all-gather.2.cloned.1.call-update) | async-done | bytes 1310736 | tf_op jit(solution)/shard_map/all_gather | solution.py:60
  156.9 9.2 %gather_fusion.2 = bf16[2304,512]{1,0:T(8,128)(2,1)} fusion(bf16[1280,512]{1,0:T(8,128)(2,1)} %all-gather.2.cloned.1.call-done, s32[3072]{0:T(1024)S(1)} %get-tuple-element.33), kind=kCustom, calls=%fused_computation.2 | custom fusion | bytes 4727808 | tf_op jit(solution)/shard_map/gather | solution.py:66
  166.1 7.5 %gather_fusion.1 = bf16[2304,512]{1,0:T(8,128)(2,1)} fusion(bf16[1280,512]{1,0:T(8,128)(2,1)S(1)} %copy-done.1, s32[3072]{0:T(1024)S(1)} %get-tuple-element.34), kind=kCustom, calls=%fused_computation.1 | custom fusion | bytes 4727808 | tf_op jit(solution)/shard_map/gather | solution.py:66
  173.6 7.5 %gather_fusion = bf16[2304,512]{1,0:T(8,128)(2,1)} fusion(bf16[1280,512]{1,0:T(8,128)(2,1)S(1)} %copy-done.1, s32[3072]{0:T(1024)S(1)} %pad_clamp_fusion.2), kind=kCustom, calls=%fused_computation | custom fusion | bytes 4727808 | tf_op jit(solution)/shard_map/gather | solution.py:66
  181.1 20.5 %all-to-all-done = bf16[32,72,739]{2,1,0:T(8,128)(2,1)} async-done(((bf16[32,72,739]{2,1,0:T(8,128)(2,1)}), bf16[32,72,739]{2,1,0:T(8,128)(2,1)}, u32[]{:S(2)}, u32[]{:S(2)}) %all-to-all-start) | async-done | bytes 3405344 | tf_op jit(solution)/shard_map/all_to_all | solution.py:49
  201.6 2.0 convolution_convert_fusion.2
  203.7 3.9 convolution_convert_fusion.1
  207.7 0.0 copy-done.5
  207.7 0.0 copy-done
  207.7 0.0 copy-done.6
  207.7 0.0 copy-done.7
  207.7 0.6 copy-done.8
  208.4 9.1 %multiply_convert_fusion = (bf16[2304,512]{1,0:T(8,128)(2,1)}, bf16[2304,512]{1,0:T(8,128)(2,1)}, bf16[2304,512]{1,0:T(8,128)(2,1)}, bf16[2304,512]{1,0:T(8,128)(2,1)}) fusion(bf16[2304,512]{1,0:T(8,128)(2,1)S(1)} %convolution_convert_fusion.1, bf16[2304,512]{1,0:T(8,128)(2,1)S(1)} %copy-done.6, bf16[2304,512]{1,0:T(8,128)(2,1)S(1)} %copy-done.7, ...), kind=kOutput, calls=%fused_computation.20 | convolution fusion | flops 1255145472 | bytes 21757952 | tf_op jit(solution)/shard_map/dot_general | solution.py:25
  217.4 17.0 %scatter_custom_fusion.1 = f32[1280,512]{1,0:T(8,128)S(1)} fusion(s32[2304]{0:T(1024)S(1)} %get-tuple-element.22, bf16[2304,512]{1,0:T(8,128)(2,1)} %get-tuple-element.30, f32[]{:T(128)} %constant.20.clone.1), kind=kCustom, calls=%fused_computation.16 | custom fusion | flops 2359296 | bytes 4980740 | tf_op jit(solution)/shard_map/scatter-add | solution.py:86
  234.5 17.5 %scatter_custom_fusion.2 = f32[1280,512]{1,0:T(8,128)S(1)} fusion(f32[1280,512]{1,0:T(8,128)S(1)} %scatter_custom_fusion.1, s32[2304]{0:T(1024)S(1)} %get-tuple-element.21, bf16[2304,512]{1,0:T(8,128)(2,1)} %get-tuple-element.28), kind=kCustom, calls=%fused_computation.14 | custom fusion | flops 2359296 | bytes 4980736 | tf_op jit(solution)/shard_map/scatter-add | solution.py:86
  252.0 17.4 %scatter_custom_fusion.3 = f32[1280,512]{1,0:T(8,128)S(1)} fusion(f32[1280,512]{1,0:T(8,128)S(1)} %scatter_custom_fusion.2, s32[2304]{0:T(1024)S(1)} %get-tuple-element.20, bf16[2304,512]{1,0:T(8,128)(2,1)} %get-tuple-element.27), kind=kCustom, calls=%fused_computation.11 | custom fusion | flops 2359296 | bytes 4980736 | tf_op jit(solution)/shard_map/scatter-add | solution.py:86
  269.4 0.0 copy-start.2
  269.4 1.5 copy-done.2
  270.9 0.0 reduce-scatter.2.cloned.1.call-update
  270.9 0.3 all-reduce.3.cloned.1.call-start
  271.2 4.8 %fusion.24 = f32[512,512]{0,1:T(8,128)} fusion(bf16[2304,512]{1,0:T(8,128)(2,1)} %get-tuple-element.29, bf16[2304,512]{1,0:T(8,128)(2,1)} %copy-done.5), kind=kOutput, calls=%fused_computation.74 | convolution fusion | flops 1207959552 | bytes 5767168 | tf_op jit(solution)/shard_map/dot_general | solution.py:19
  275.9 5.0 %fusion.12 = f32[512,227]{0,1:T(8,128)} fusion(bf16[2304,739]{1,0:T(8,128)(2,1)} %bitcast.2, bf16[2304,512]{1,0:T(8,128)(2,1)} %get-tuple-element.29, bf16[512,512]{1,0:T(8,128)(2,1)S(1)} %copy-done), kind=kOutput, calls=%fused_computation.37 | convolution fusion | flops 1744699392 | bytes 4528128 | tf_op jit(solution)/shard_map/dot_general | solution.py:19
  280.9 5.5 %fusion.7 = f32[512,512]{0,1:T(8,128)} fusion(bf16[2304,512]{1,0:T(8,128)(2,1)} %get-tuple-element.27, bf16[2304,512]{1,0:T(8,128)(2,1)} %get-tuple-element.28, bf16[2304,512]{1,0:T(8,128)(2,1)S(1)} %copy-done.4, bf16[2304,739]{1,0:T(8,128)(2,1)} %bitcast.2), kind=kOutput, calls=%fused_computation.29 | convolution fusion | flops 1215037440 | bytes 10485760 | tf_op jit(solution)/shard_map/dot_general | solution.py:19
  286.5 19.3 %reduce-scatter.2.cloned.1.call-done = f32[320,512]{1,0:T(8,128)} async-done(((f32[1280,512]{1,0:T(8,128)}), f32[320,512]{1,0:T(8,128)}) %reduce-scatter.2.cloned.1.call-update) | async-done | bytes 655376 | tf_op jit(solution)/shard_map/reduce_scatter | solution.py:87
  305.8 2.6 convolution_bitcast_fusion
  308.4 0.0 all-reduce.3.cloned.1.call-update
  308.4 1.1 convolution_convert_fusion.3
  309.5 143.8 %all-reduce.3.cloned.1.call-done = (f32[512,512]{0,1:T(8,128)}, f32[512,512]{0,1:T(8,128)}, f32[512,512]{0,1:T(8,128)}, f32[512,227]{0,1:T(8,128)}) async-done(((f32[512,512]{0,1:T(8,128)}, f32[512,512]{0,1:T(8,128)}, f32[512,512]{0,1:T(8,128)}, f32[512,227]{0,1:T(8,128)}), (f32[512,512]{0,1:T(8,128)}, f32[512,512]{0,1:T(8,128)}, f32[512,512]{0,1:T(8,128)}, ...) | async-done | bytes 3610640 | tf_op jit(solution)/shard_map/psum | solution.py:94
  453.3 1.4 broadcast_multiply_fusion.2
  454.7 1.3 copy.29
  456.0 0.8 broadcast_multiply_fusion.3
  456.8 1.3 broadcast_multiply_fusion.1
  458.2 1.3 copy.30
  459.5 0.1 broadcast_multiply_fusion
  459.6 1.3 copy.31
  (31 shorter events, 0.1 us)
Async XLA Ops:
  7.2 200.5 %copy-start = (bf16[512,512]{1,0:T(8,128)(2,1)S(1)}, bf16[512,512]{1,0:T(8,128)(2,1)}, u32[]{:S(2)}) copy-start(bf16[512,512]{1,0:T(8,128)(2,1)} %param.16) | copy-start | bytes 1572868
  114.1 7.5 %copy-start.9 = (bf16[512,512]{1,0:T(8,128)(2,1)S(1)}, bf16[512,512]{1,0:T(8,128)(2,1)}, u32[]{:S(2)}) copy-start(bf16[512,512]{1,0:T(8,128)(2,1)} %param.14) | copy-start | bytes 1572868
  114.1 7.5 %copy-start.11 = (bf16[320,512]{1,0:T(8,128)(2,1)S(1)}, bf16[320,512]{1,0:T(8,128)(2,1)}, u32[]{:S(2)}) copy-start(bf16[320,512]{1,0:T(8,128)(2,1)} %param.11) | copy-start | bytes 983044
  114.1 8.7 %copy-start.15 = (s32[3,2304]{1,0:T(4,128)S(1)}, s32[3,2304]{1,0:T(4,128)}, u32[]{:S(2)}) copy-start(s32[3,2304]{1,0:T(4,128)} %param.13) | copy-start | bytes 82948
  114.1 87.5 %all-to-all-start = ((bf16[32,72,739]{2,1,0:T(8,128)(2,1)}), bf16[32,72,739]{2,1,0:T(8,128)(2,1)}, u32[]{:S(2)}, u32[]{:S(2)}) async-start(bf16[32,72,739]{2,1,0:T(8,128)(2,1)} %scatter_fusion), calls=%async_computation | async-start | bytes 7077888 | tf_op jit(solution)/shard_map/all_to_all | solution.py:49
  121.6 35.3 %all-gather.2.cloned.1.call-start = ((), (), s32[]{:S(2)}) async-start(), calls=%async_computation.2 | async-start | bytes 1638400 | tf_op jit(solution)/shard_map/all_gather | solution.py:60
  122.7 183.0 %reduce-scatter.2.cloned.1.call-start = ((), (), s32[]{:S(2)}) async-start(), calls=%async_computation.3 | async-start | bytes 3276800 | tf_op jit(solution)/shard_map/reduce_scatter | solution.py:87
  156.9 9.2 %copy-start.1 = (bf16[1280,512]{1,0:T(8,128)(2,1)S(1)}, bf16[1280,512]{1,0:T(8,128)(2,1)}, u32[]{:S(2)}) copy-start(bf16[1280,512]{1,0:T(8,128)(2,1)} %all-gather.2.cloned.1.call-done) | copy-start | bytes 3932164
  173.6 28.0 %copy-start.14 = (bf16[512,227]{0,1:T(8,128)(2,1)S(1)}, bf16[512,227]{0,1:T(8,128)(2,1)}, u32[]{:S(2)}) copy-start(bf16[512,227]{0,1:T(8,128)(2,1)} %param.17) | copy-start | bytes 697348
  181.1 22.6 %copy-start.16 = (bf16[512,512]{1,0:T(8,128)(2,1)S(1)}, bf16[512,512]{1,0:T(8,128)(2,1)}, u32[]{:S(2)}) copy-start(bf16[512,512]{1,0:T(8,128)(2,1)} %param.15) | copy-start | bytes 1572868
  203.7 4.0 copy-start.5
  203.7 4.0 copy-start.6
  203.7 4.0 copy-start.7
  203.7 4.6 copy-start.8
  269.4 1.5 copy-start.2
  270.9 182.4 %all-reduce.3.cloned.1.call-start = ((), (), s32[]{:S(2)}) async-start(), calls=%async_computation.4 | async-start | bytes 7241728 | tf_op jit(solution)/shard_map/psum | solution.py:94
  275.9 5.0 %copy-start.4 = (bf16[2304,512]{1,0:T(8,128)(2,1)S(1)}, bf16[2304,512]{1,0:T(8,128)(2,1)}, u32[]{:S(2)}) copy-start(bf16[2304,512]{1,0:T(8,128)(2,1)} %get-tuple-element.30) | copy-start | bytes 7077892
  286.5 21.9 %copy-start.10 = (bf16[512,512]{1,0:T(8,128)(2,1)S(1)}, bf16[512,512]{1,0:T(8,128)(2,1)}, u32[]{:S(2)}) copy-start(bf16[512,512]{1,0:T(8,128)(2,1)} %param.14) | copy-start | bytes 1572868
  305.8 2.6 copy-start.3
  453.3 2.7 copy-start.13
  456.0 3.5 copy-start.12
Sparse Core Ops, SparseCore 0:
  124.5 32.3 all-gather.1
  271.0 34.7 reduce-scatter.1
  312.4 140.8 all-reduce.2
where the time goes:
time: 472 us; the launch traced here: 467 us
  waiting for transfers between devices  218 us (46%)
  local copies, waits for them, and re-layouts  134 us (28%)
  other arithmetic  58.8 us (12%)
  matrix products  35.1 us (7%)
  between operations  14 us (3%)
  starting transfers between devices  7.79 us (2%)
    psum x1, waiting for transfers between devices, shards(): mesh_total = lax.psum(mesh_part, ('band', 'sub'))  144 us
    scatter x1, local copies, waits for them, and re-layouts, shards(): jnp.zeros((devices, capacity, row_width), jnp.bfloat16)  102 us
    scatter-add x3, other arithmetic, shards(): node_part.at[local_node[corner]].add(pre_grads[corner].astype(jnp.float32))  51.9 us
    all_gather x1, waiting for transfers between devices, shards(): patch_proj = lax.all_gather(mesh_proj, 'sub', axis=0, tiled=True)  33.9 us
    gather x3, local copies, waits for them, and re-layouts, shards(): patch_proj[local_node[corner]].astype(jnp.float32) + grid_float  24.2 us
    all_to_all x1, waiting for transfers between devices, shards(): lax.all_to_all(send_buffer, ('band', 'sub'), split_axis=0, concat_axis=0,...  20.5 us
    reduce_scatter x1, waiting for transfers between devices, shards(): lax.psum_scatter(node_part, 'sub', scatter_dimension=0, tiled=True)  19.3 us
    dot_general x4, matrix products, contract_rows(): lax.dot_general(left, right, (((0,), (0,)), ((), ())), preferred_element_...  17.9 us
  transfers between devices with their start and end apart: 4, of which 4 were waited for; matrix products, arithmetic and copies ran while one was open for 9% of the time, Pallas kernels for 0%

commit v1 on v0

--- a/solution.py
+++ b/solution.py
@@ -91,7 +91,7 @@
     mesh_part = contract_rows(mesh_latent, mesh_proj_grad)
     grad_scale = 1.0 / math.sqrt(3.0 * total_points)
     grid_total = lax.psum(grid_part, ("band", "sub"))
-    mesh_total = lax.psum(mesh_part, ("band", "sub"))
+    mesh_total = lax.all_gather(mesh_part, axis_name=("band", "sub")).sum(axis=0)
     return (
         mesh_grad,
         mesh_total * grad_scale,

time: 472 us -> 701 us (1.49)
  waiting for transfers between devices: 218 us -> 409 us
  local copies, waits for them, and re-layouts: 134 us -> 163 us
  other arithmetic: 58.8 us -> 66.9 us
    all_gather x0 -> x1, waiting for transfers between devices: none -> 195 us  [shards(): lax.all_gather(mesh_part, axis_name=('band', 'sub')).sum(axis=0)]
    unnamed x37 -> x33, local copies, waits for them, and re-layouts: 6.12 us -> 34.7 us
  transfers between devices with their start and end apart: 4 -> 5, of which waited for: 4 -> 5; matrix products, arithmetic and copies ran while one was open for 9% -> 7% of each run, Pallas kernels for 0% -> 0%
where the time goes in v1:
time: 701 us; the launch traced here: 696 us
  waiting for transfers between devices  409 us (58%)
  local copies, waits for them, and re-layouts  163 us (23%)
  other arithmetic  66.9 us (10%)
  matrix products  35.2 us (5%)
  between operations  14 us (2%)
  starting transfers between devices  7.88 us (1%)
    all_gather x1, waiting for transfers between devices, shards(): lax.all_gather(mesh_part, axis_name=('band', 'sub')).sum(axis=0)  195 us
    psum x1, waiting for transfers between devices, shards(): grid_total = lax.psum(grid_part, ('band', 'sub'))  141 us
    scatter x1, local copies, waits for them, and re-layouts, shards(): jnp.zeros((devices, capacity, row_width), jnp.bfloat16)  101 us
    scatter-add x3, other arithmetic, shards(): node_part.at[local_node[corner]].add(pre_grads[corner].astype(jnp.float32))  51.9 us
    unnamed x33, local copies, waits for them, and re-layouts  34.7 us
    all_gather x1, waiting for transfers between devices, shards(): patch_proj = lax.all_gather(mesh_proj, 'sub', axis=0, tiled=True)  33.9 us
    gather x3, local copies, waits for them, and re-layouts, shards(): patch_proj[local_node[corner]].astype(jnp.float32) + grid_float  24.2 us
    all_to_all x1, waiting for transfers between devices, shards(): lax.all_to_all(send_buffer, ('band', 'sub'), split_axis=0, concat_axis=0,...  20.5 us
  transfers between devices with their start and end apart: 5, of which 5 were waited for; matrix products, arithmetic and copies ran while one was open for 7% of the time, Pallas kernels for 0%

profile of v1, /device:TPU:0, one launch (start us, length us, event | category | flops | bytes accessed | tf_op | source)
XLA Modules:
  0.0 696.4 jit_solution(13431130467066327387)
XLA Ops:
  7.2 0.0 copy-start
  7.2 0.8 compare_select_fusion.4
  8.0 1.0 fusion.15
  9.0 0.2 copy.18
  9.2 1.2 pad_maximum_fusion
  10.5 2.0 broadcast_in_dim.9
  12.5 101.4 %scatter_fusion = bf16[32,72,739]{2,1,0:T(8,128)(2,1)} fusion(bf16[32,72,739]{2,1,0:T(8,128)(2,1)} %broadcast_in_dim.9, s32[768]{0:T(1024)S(1)} %fusion.23, bf16[768,739]{1,0:T(8,128)(2,1)S(1)} %pad_maximum_fusion), kind=kCustom, calls=%fused_computation.3 | custom fusion | bytes 3411456 | tf_op jit(solution)/shard_map/scatter | solution.py:47
  114.0 7.5 %all-to-all-start = ((bf16[32,72,739]{2,1,0:T(8,128)(2,1)}), bf16[32,72,739]{2,1,0:T(8,128)(2,1)}, u32[]{:S(2)}, u32[]{:S(2)}) async-start(bf16[32,72,739]{2,1,0:T(8,128)(2,1)} %scatter_fusion), calls=%async_computation | async-start | bytes 7077888 | tf_op jit(solution)/shard_map/all_to_all | solution.py:49
  121.5 0.0 all-gather.4.cloned.1.call-start
  121.5 1.1 convolution_convert_fusion.4
  122.6 0.0 all-gather.4.cloned.1.call-update
  122.6 0.0 reduce-scatter.2.cloned.1.call-start
  122.7 0.0 copy-done.14
  122.7 0.1 fusion.20
  122.8 33.9 %all-gather.4.cloned.1.call-done = bf16[1280,512]{1,0:T(8,128)(2,1)} async-done(((bf16[320,512]{1,0:T(8,128)(2,1)}), bf16[1280,512]{1,0:T(8,128)(2,1)}) %all-gather.4.cloned.1.call-update) | async-done | bytes 1310736 | tf_op jit(solution)/shard_map/all_gather | solution.py:60
  156.8 9.2 %gather_fusion.2 = bf16[2304,512]{1,0:T(8,128)(2,1)} fusion(bf16[1280,512]{1,0:T(8,128)(2,1)} %all-gather.4.cloned.1.call-done, s32[3072]{0:T(1024)S(1)} %get-tuple-element.17), kind=kCustom, calls=%fused_computation.2 | custom fusion | bytes 4727808 | tf_op jit(solution)/shard_map/gather | solution.py:66
  166.0 7.5 %gather_fusion.1 = bf16[2304,512]{1,0:T(8,128)(2,1)} fusion(bf16[1280,512]{1,0:T(8,128)(2,1)S(1)} %copy-done.1, s32[3072]{0:T(1024)S(1)} %get-tuple-element.18), kind=kCustom, calls=%fused_computation.1 | custom fusion | bytes 4727808 | tf_op jit(solution)/shard_map/gather | solution.py:66
  173.5 7.5 %gather_fusion = bf16[2304,512]{1,0:T(8,128)(2,1)} fusion(bf16[1280,512]{1,0:T(8,128)(2,1)S(1)} %copy-done.1, s32[3072]{0:T(1024)S(1)} %pad_clamp_fusion.2), kind=kCustom, calls=%fused_computation | custom fusion | bytes 4727808 | tf_op jit(solution)/shard_map/gather | solution.py:66
  181.0 20.5 %all-to-all-done = bf16[32,72,739]{2,1,0:T(8,128)(2,1)} async-done(((bf16[32,72,739]{2,1,0:T(8,128)(2,1)}), bf16[32,72,739]{2,1,0:T(8,128)(2,1)}, u32[]{:S(2)}, u32[]{:S(2)}) %all-to-all-start) | async-done | bytes 3405344 | tf_op jit(solution)/shard_map/all_to_all | solution.py:49
  201.5 2.0 convolution_convert_fusion.2
  203.6 3.9 convolution_convert_fusion.1
  207.6 0.6 copy-done.8
  208.2 9.1 %multiply_convert_fusion = (bf16[2304,512]{1,0:T(8,128)(2,1)}, bf16[2304,512]{1,0:T(8,128)(2,1)}, bf16[2304,512]{1,0:T(8,128)(2,1)}, bf16[2304,512]{1,0:T(8,128)(2,1)}) fusion(bf16[2304,512]{1,0:T(8,128)(2,1)S(1)} %convolution_convert_fusion.1, bf16[2304,512]{1,0:T(8,128)(2,1)S(1)} %copy-done.6, bf16[2304,512]{1,0:T(8,128)(2,1)S(1)} %copy-done.7, ...), kind=kOutput, calls=%fused_computation.21 | convolution fusion | flops 1255145472 | bytes 21757952 | tf_op jit(solution)/shard_map/dot_general | solution.py:25
  217.3 17.0 %scatter_custom_fusion.1 = f32[1280,512]{1,0:T(8,128)S(1)} fusion(s32[2304]{0:T(1024)S(1)} %get-tuple-element.7, bf16[2304,512]{1,0:T(8,128)(2,1)} %get-tuple-element.14, f32[]{:T(128)} %constant.20.clone.1), kind=kCustom, calls=%fused_computation.17 | custom fusion | flops 2359296 | bytes 4980740 | tf_op jit(solution)/shard_map/scatter-add | solution.py:86
  234.3 17.5 %scatter_custom_fusion.2 = f32[1280,512]{1,0:T(8,128)S(1)} fusion(f32[1280,512]{1,0:T(8,128)S(1)} %scatter_custom_fusion.1, s32[2304]{0:T(1024)S(1)} %get-tuple-element.6, bf16[2304,512]{1,0:T(8,128)(2,1)} %get-tuple-element.12), kind=kCustom, calls=%fused_computation.15 | custom fusion | flops 2359296 | bytes 4980736 | tf_op jit(solution)/shard_map/scatter-add | solution.py:86
  251.9 17.4 %scatter_custom_fusion.3 = f32[1280,512]{1,0:T(8,128)S(1)} fusion(f32[1280,512]{1,0:T(8,128)S(1)} %scatter_custom_fusion.2, s32[2304]{0:T(1024)S(1)} %get-tuple-element.5, bf16[2304,512]{1,0:T(8,128)(2,1)} %get-tuple-element.11), kind=kCustom, calls=%fused_computation.12 | custom fusion | flops 2359296 | bytes 4980736 | tf_op jit(solution)/shard_map/scatter-add | solution.py:86
  269.2 1.5 copy-done.2
  270.7 0.0 reduce-scatter.2.cloned.1.call-update
  270.8 0.0 all-reduce.3.cloned.1.call-start
  270.8 4.8 fusion.24
  275.6 5.2 fusion.12
  280.8 5.5 fusion.7
  286.3 0.0 all-reduce.3.cloned.1.call-update
  286.4 0.3 all-gather.6.cloned.1.call-start
  286.6 19.0 %reduce-scatter.2.cloned.1.call-done = f32[320,512]{1,0:T(8,128)} async-done(((f32[1280,512]{1,0:T(8,128)}), f32[320,512]{1,0:T(8,128)}) %reduce-scatter.2.cloned.1.call-update) | async-done | bytes 655376 | tf_op jit(solution)/shard_map/reduce_scatter | solution.py:87
  305.7 2.5 convolution_bitcast_fusion
  308.2 0.0 all-gather.6.cloned.1.call-update
  308.2 0.0 copy-start.10
  308.2 141.0 %all-reduce.3.cloned.1.call-done = (f32[512,512]{1,0:T(8,128)}, f32[512,512]{1,0:T(8,128)}, f32[512,227]{0,1:T(8,128)}) async-done(((f32[512,512]{1,0:T(8,128)}, f32[512,512]{1,0:T(8,128)}, f32[512,227]{0,1:T(8,128)}), (f32[512,512]{1,0:T(8,128)}, f32[512,512]{1,0:T(8,128)}, f32[512,227]{0,1:T(8,128)})) %all-reduce.3.cloned.1.call-update) | async-done | bytes 2562064 | tf_op jit(solution)/shard_map/psum | solution.py:93
  449.2 1.9 broadcast_multiply_fusion.3
  451.1 2.3 broadcast_multiply_fusion.1
  453.4 1.1 broadcast_multiply_fusion
  454.5 1.1 convolution_convert_fusion.3
  455.6 194.9 %all-gather.6.cloned.1.call-done = f32[16384,512]{0,1:T(8,128)} async-done(((f32[512,512]{0,1:T(8,128)}), f32[16384,512]{0,1:T(8,128)}) %all-gather.6.cloned.1.call-update) | async-done | bytes 33554448 | tf_op jit(solution)/shard_map/all_gather | solution.py:94
  650.5 32.5 %copy.20 = f32[64,8,32,512]{3,2,1,0:T(8,128)S(1)} copy(f32[64,8,32,512]{3,1,2,0:T(8,128)} %bitcast.35) | data formatting | bytes 67108864
  683.1 5.4 bitcast_reduce_fusion
  688.4 0.3 copy.19
  688.8 1.1 broadcast_multiply_fusion.2
  (32 shorter events, 0.2 us)
Async XLA Ops:
  7.2 200.4 %copy-start = (bf16[512,512]{1,0:T(8,128)(2,1)S(1)}, bf16[512,512]{1,0:T(8,128)(2,1)}, u32[]{:S(2)}) copy-start(bf16[512,512]{1,0:T(8,128)(2,1)} %param.16) | copy-start | bytes 1572868
  113.9 7.6 %copy-start.9 = (bf16[512,512]{1,0:T(8,128)(2,1)S(1)}, bf16[512,512]{1,0:T(8,128)(2,1)}, u32[]{:S(2)}) copy-start(bf16[512,512]{1,0:T(8,128)(2,1)} %param.14) | copy-start | bytes 1572868
  113.9 7.6 %copy-start.11 = (bf16[320,512]{1,0:T(8,128)(2,1)S(1)}, bf16[320,512]{1,0:T(8,128)(2,1)}, u32[]{:S(2)}) copy-start(bf16[320,512]{1,0:T(8,128)(2,1)} %param.11) | copy-start | bytes 983044
  113.9 8.7 %copy-start.14 = (s32[3,2304]{1,0:T(4,128)S(1)}, s32[3,2304]{1,0:T(4,128)}, u32[]{:S(2)}) copy-start(s32[3,2304]{1,0:T(4,128)} %param.13) | copy-start | bytes 82948
  114.0 87.6 %all-to-all-start = ((bf16[32,72,739]{2,1,0:T(8,128)(2,1)}), bf16[32,72,739]{2,1,0:T(8,128)(2,1)}, u32[]{:S(2)}, u32[]{:S(2)}) async-start(bf16[32,72,739]{2,1,0:T(8,128)(2,1)} %scatter_fusion), calls=%async_computation | async-start | bytes 7077888 | tf_op jit(solution)/shard_map/all_to_all | solution.py:49
  121.5 35.3 %all-gather.4.cloned.1.call-start = ((), (), s32[]{:S(2)}) async-start(), calls=%async_computation.2 | async-start | bytes 1638400 | tf_op jit(solution)/shard_map/all_gather | solution.py:60
  122.6 183.1 %reduce-scatter.2.cloned.1.call-start = ((), (), s32[]{:S(2)}) async-start(), calls=%async_computation.3 | async-start | bytes 3276800 | tf_op jit(solution)/shard_map/reduce_scatter | solution.py:87
  156.8 9.2 %copy-start.1 = (bf16[1280,512]{1,0:T(8,128)(2,1)S(1)}, bf16[1280,512]{1,0:T(8,128)(2,1)}, u32[]{:S(2)}) copy-start(bf16[1280,512]{1,0:T(8,128)(2,1)} %all-gather.4.cloned.1.call-done) | copy-start | bytes 3932164
  173.5 28.0 %copy-start.13 = (bf16[512,227]{0,1:T(8,128)(2,1)S(1)}, bf16[512,227]{0,1:T(8,128)(2,1)}, u32[]{:S(2)}) copy-start(bf16[512,227]{0,1:T(8,128)(2,1)} %param.17) | copy-start | bytes 697348
  181.0 22.6 %copy-start.15 = (bf16[512,512]{1,0:T(8,128)(2,1)S(1)}, bf16[512,512]{1,0:T(8,128)(2,1)}, u32[]{:S(2)}) copy-start(bf16[512,512]{1,0:T(8,128)(2,1)} %param.15) | copy-start | bytes 1572868
  203.6 4.0 copy-start.5
  203.6 4.0 copy-start.6
  203.6 4.0 copy-start.7
  203.6 4.6 copy-start.8
  269.2 1.5 copy-start.2
  270.8 178.4 %all-reduce.3.cloned.1.call-start = ((), (), s32[]{:S(2)}) async-start(), calls=%async_computation.5 | async-start | bytes 5144576 | tf_op jit(solution)/shard_map/psum | solution.py:93
  275.6 5.2 copy-start.4
  286.4 364.2 %all-gather.6.cloned.1.call-start = ((), (), s32[]{:S(2)}) async-start(), calls=%async_computation.4 | async-start | bytes 34603008 | tf_op jit(solution)/shard_map/all_gather | solution.py:94
  308.2 146.3 %copy-start.3 = (f32[320,512]{1,0:T(8,128)S(1)}, f32[320,512]{1,0:T(8,128)}, u32[]{:S(2)}) copy-start(f32[320,512]{1,0:T(8,128)} %reduce-scatter.2.cloned.1.call-done) | copy-start | bytes 1966084
  308.2 146.3 %copy-start.10 = (bf16[512,512]{1,0:T(8,128)(2,1)S(1)}, bf16[512,512]{1,0:T(8,128)(2,1)}, u32[]{:S(2)}) copy-start(bf16[512,512]{1,0:T(8,128)(2,1)} %param.14) | copy-start | bytes 1572868
  449.2 4.2 copy-start.12
Sparse Core Ops, SparseCore 0:
  124.4 32.3 all-gather.3
  270.9 34.7 reduce-scatter.1
  312.1 137.0 all-reduce.2
  452.6 197.9 all-gather.5
